TPU v7x, 32 devices: a whole 2x2x4 slice. The times are simulated.
32 devices in a mesh: lat: 4 (over y, core), lon: 4 (over z), lev: 2 (over x).
Axes of the slice: x: 2, y: 2, z: 4, core: 2. Of those that a mesh axis runs over, the one named last changes fastest.
Arguments:
- density: float32 [128, 16, 256, 128], P('lat', 'lon', 'lev'), may hold values from 0.2 to 1.8
- crowding: float32 [128, 16, 256, 128], P('lat', 'lon', 'lev'), may hold values from 0.5 to 2
Outputs:
- running_total: float32 [128, 16, 256, 128], P('lat', 'lon', 'lev')
- density_end: float32 [128, 16, 256, 128], P('lat', 'lon', 'lev')
All inputs are finite; a program needn't handle non-finite values.
Results may differ from a plain program's by a relative error of at most 0.00002.
Values sent between devices are 32-bit elements; how exact they have to be, the bound alone decides.
A program may use at most 320 MiB of HBM per device.

v0:
```python
import jax
import jax.numpy as jnp
from jax import lax
from jax.sharding import PartitionSpec as P

STEPS = 4


def with_halo(cells, sides, width):
    for axis, dim in sides:
        count = lax.axis_size(axis)
        head = lax.slice_in_dim(cells, 0, width, axis=dim)
        tail = lax.slice_in_dim(cells, cells.shape[dim] - width, cells.shape[dim], axis=dim)
        cells = jnp.concatenate(
            [
                lax.ppermute(tail, axis, [(i, (i + 1) % count) for i in range(count)]),
                cells,
                lax.ppermute(head, axis, [((i + 1) % count, i) for i in range(count)]),
            ],
            axis=dim,
        )
    return cells


def carried_in(value, axis, join, neutral):
    count, mine = (lax.axis_size(axis), lax.axis_index(axis))
    pieces = lax.all_gather(value, axis)
    so_far = jnp.full_like(value, 0) + jnp.asarray(neutral, value.dtype)

    def lap(position, so_far):
        longer = join(so_far, pieces[position])
        return jnp.where(position < mine, longer, so_far)

    return lax.fori_loop(0, count - 1, lap, so_far)


def without_rim(values, dims):
    for dim in dims:
        values = lax.slice_in_dim(values, 1, values.shape[dim] - 1, axis=dim)
    return values


def shifted_cells(values, dim, start, dims):
    others = [other for other in dims if other != dim]
    values = without_rim(values, others)
    return lax.slice_in_dim(values, start, start + values.shape[dim] - 2, axis=dim)


def march_step(padded, crowding):
    middle = without_rim(padded, (0, 1, 2))
    lower = [shifted_cells(padded, dim, 0, (0, 1, 2)) for dim in (0, 1, 2)]
    upper = [shifted_cells(padded, dim, 2, (0, 1, 2)) for dim in (0, 1, 2)]
    spread = lower[0] + upper[0] + lower[1] + upper[1] + lower[2] + upper[2] - 6.0 * middle
    return middle + 0.1 * spread + 0.2 * middle * (1.0 - middle * crowding)


def body(density, crowding):
    for step in range(STEPS):
        padded = with_halo(density, (("lat", 0), ("lon", 1), ("lev", 2)), 1)
        density = march_step(padded, crowding)
    here = jnp.cumsum(density, axis=1)
    total = lax.slice_in_dim(here, here.shape[1] - 1, here.shape[1], axis=1)

    def add_pair(earlier_total, later_total):
        return earlier_total + later_total

    below = carried_in(total, "lon", add_pair, jnp.zeros_like(total))
    running_total = (here + below) / (density.shape[1] * lax.axis_size("lon"))
    return (running_total, density)


def solution(mesh):
    return jax.shard_map(
        body,
        mesh=mesh,
        in_specs=(P("lat", "lon", "lev", None), P("lat", "lon", "lev", None)),
        out_specs=(P("lat", "lon", "lev", None), P("lat", "lon", "lev", None)),
        check_vma=False,
    )
```

profile of v0, /device:TPU:24, one launch (start us, length us, event | category | flops | bytes accessed | tf_op | source)
XLA Modules:
  0.0 769.1 jit_solution(18261941237726202400)
XLA Ops:
  10.1 5.0 collective-permute-done
  15.1 4.0 constant_dynamic-update-slice_fusion.1
  21.8 96.2 %collective-permute-done.2 = f32[34,1,128,128]{3,2,1,0:T(8,128)S(1)} collective-permute-done((f32[34,1,128,128]{3,2,1,0:T(8,128)S(1)}, f32[34,1,128,128]{3,2,1,0:T(8,128)S(1)}, u32[]{:S(2)}, u32[]{:S(2)}) %collective-permute-start.2) | collective-permute-done | bytes 2228256 | tf_op jit(solution)/shard_map/ppermute | solution.py:16
  120.4 3.6 collective-permute-done.4
  125.3 30.1 %fusion.31 = f32[32,4,128,128]{3,2,1,0:T(8,128)S(1)} fusion(f32[32,4,128,128]{3,2,1,0:T(8,128)} %param.4, f32[34,6,1,128]{3,2,1,0:T(1,128)S(1)} %copy.26, f32[34,1,128,128]{3,2,1,0:T(8,128)} %copy-done.6, f32[34,4,128,128]{3,2,1,0:T(8,128)} %copy-done.2, f32[34,1,128,128]{3,2,1,0:T(8,128)S(1)} %collective-permute-done.2, f32[34,6,1,128]{3,2,1,0:T(1,128)S(1)} %copy.24, ...), kind=kLoop, calls=%fused_computation.87 | loop fusion | flops 50331648 | bytes 39268352 | tf_op jit(solution)/shard_map/add | solution.py:54
  157.3 6.1 collective-permute-done.6
  166.2 48.8 %collective-permute-done.8 = f32[34,1,128,128]{3,2,1,0:T(8,128)S(1)} collective-permute-done((f32[34,1,128,128]{3,2,1,0:T(8,128)S(1)}, f32[34,1,128,128]{3,2,1,0:T(8,128)S(1)}, u32[]{:S(2)}, u32[]{:S(2)}) %collective-permute-start.8) | collective-permute-done | bytes 2228256 | tf_op jit(solution)/shard_map/ppermute | solution.py:16
  215.0 48.5 %collective-permute-done.9 = f32[34,1,128,128]{3,2,1,0:T(8,128)S(1)} collective-permute-done((f32[34,1,128,128]{3,2,1,0:T(8,128)S(1)}, f32[34,1,128,128]{3,2,1,0:T(8,128)S(1)}, u32[]{:S(2)}, u32[]{:S(2)}) %collective-permute-start.9) | collective-permute-done | bytes 2228256 | tf_op jit(solution)/shard_map/ppermute | solution.py:18
  265.8 3.8 collective-permute-done.10
  271.1 32.7 %fusion.22 = f32[32,4,128,128]{3,2,1,0:T(8,128)S(1)} fusion(f32[32,4,128,128]{3,2,1,0:T(8,128)} %copy-done.1, f32[34,6,1,128]{3,2,1,0:T(1,128)S(1)} %copy.30, f32[34,1,128,128]{3,2,1,0:T(8,128)} %copy-done.7, f32[34,1,128,128]{3,2,1,0:T(8,128)} %copy-done.3, f32[1,4,128,128]{3,2,1,0:T(8,128)S(1)} %collective-permute-done.7, ...), kind=kLoop, calls=%fused_computation.60 | loop fusion | flops 67108864 | bytes 30355456 | tf_op jit(solution)/shard_map/add | solution.py:54
  305.8 5.5 collective-permute-done.12
  314.6 48.9 %collective-permute-done.14 = f32[34,1,128,128]{3,2,1,0:T(8,128)S(1)} collective-permute-done((f32[34,1,128,128]{3,2,1,0:T(8,128)S(1)}, f32[34,1,128,128]{3,2,1,0:T(8,128)S(1)}, u32[]{:S(2)}, u32[]{:S(2)}) %collective-permute-start.14) | collective-permute-done | bytes 2228256 | tf_op jit(solution)/shard_map/ppermute | solution.py:16
  363.5 48.5 %collective-permute-done.15 = f32[34,1,128,128]{3,2,1,0:T(8,128)S(1)} collective-permute-done((f32[34,1,128,128]{3,2,1,0:T(8,128)S(1)}, f32[34,1,128,128]{3,2,1,0:T(8,128)S(1)}, u32[]{:S(2)}, u32[]{:S(2)}) %collective-permute-start.15) | collective-permute-done | bytes 2228256 | tf_op jit(solution)/shard_map/ppermute | solution.py:18
  415.5 4.1 collective-permute-done.16
  421.3 23.2 %fusion.13 = f32[32,4,128,128]{3,2,1,0:T(8,128)} fusion(f32[32,4,128,128]{3,2,1,0:T(8,128)S(1)} %fusion.22, f32[34,6,1,128]{3,2,1,0:T(1,128)S(1)} %copy.34, f32[34,1,128,128]{3,2,1,0:T(8,128)} %copy-done.8, f32[34,1,128,128]{3,2,1,0:T(8,128)} %copy-done.4, f32[1,4,128,128]{3,2,1,0:T(8,128)S(1)} %collective-permute-done.13, ...), kind=kLoop, calls=%fused_computation.33 | loop fusion | flops 67108864 | bytes 30355456 | tf_op jit(solution)/shard_map/add | solution.py:54
  447.5 5.8 collective-permute-done.18
  458.2 97.0 %collective-permute-done.20 = f32[34,1,128,128]{3,2,1,0:T(8,128)S(1)} collective-permute-done((f32[34,1,128,128]{3,2,1,0:T(8,128)S(1)}, f32[34,1,128,128]{3,2,1,0:T(8,128)S(1)}, u32[]{:S(2)}, u32[]{:S(2)}) %collective-permute-start.20) | collective-permute-done | bytes 2228256 | tf_op jit(solution)/shard_map/ppermute | solution.py:16
  560.1 4.1 collective-permute-done.22
  566.0 23.2 %fusion.4 = f32[32,4,128,128]{3,2,1,0:T(8,128)} fusion(f32[32,4,128,128]{3,2,1,0:T(8,128)S(1)} %copy-done, f32[34,6,1,128]{3,2,1,0:T(1,128)S(1)} %copy.38, f32[34,1,128,128]{3,2,1,0:T(8,128)} %copy-done.9, f32[34,1,128,128]{3,2,1,0:T(8,128)} %copy-done.5, f32[1,4,128,128]{3,2,1,0:T(8,128)S(1)} %collective-permute-done.19, ...), kind=kLoop, calls=%fused_computation.6 | loop fusion | flops 67108864 | bytes 30355456 | tf_op jit(solution)/shard_map/add | solution.py:54
  589.2 8.4 %fusion.41 = f32[32,4,128,128]{3,2,1,0:T(8,128)} fusion(f32[32,4,128,128]{3,2,1,0:T(8,128)} %fusion.4), kind=kOutput, calls=%fused_computation.137 | output fusion | flops 6291456 | bytes 16777216 | tf_op jit(solution)/shard_map/jit(cumsum)/reduce_window_sum | solution.py:61
  597.6 3.1 slice.360
  600.8 145.8 %all-gather.3.cloned.1.call-done = f32[128,1,128,128]{3,2,1,0:T(8,128)} async-done(((f32[32,1,128,128]{3,2,1,0:T(8,128)}), f32[128,1,128,128]{3,2,1,0:T(8,128)}) %all-gather.3.cloned.1.call-update) | async-done | bytes 8388624 | tf_op jit(solution)/shard_map/all_gather | solution.py:27
  746.6 7.0 while.14
  753.6 8.7 %add_multiply_fusion = f32[32,4,128,128]{3,2,1,0:T(8,128)} fusion(f32[32,4,128,128]{3,2,1,0:T(8,128)} %fusion.41, f32[32,128,128]{2,1,0:T(8,128)S(1)} %bitcast.9), kind=kLoop, calls=%fused_computation.101 | loop fusion | flops 4194304 | bytes 18874368 | tf_op jit(solution)/shard_map/div | solution.py:68
  (90 shorter events, 49.7 us)
Async XLA Ops:
  7.2 739.4 %all-gather.3.cloned.1.call-start = ((), (), s32[]{:S(2)}) async-start(), calls=%async_computation | async-start | bytes 10485760 | tf_op jit(solution)/shard_map/all_gather | solution.py:27
  8.3 6.8 collective-permute-start
  8.3 10.8 %collective-permute-start.1 = (f32[1,4,128,128]{3,2,1,0:T(8,128)S(1)}, f32[1,4,128,128]{3,2,1,0:T(8,128)S(1)}, u32[]{:S(2)}, u32[]{:S(2)}) collective-permute-start(f32[1,4,128,128]{3,2,1,0:T(8,128)S(1)} %get-tuple-element.141), channel_id=1, source_target_pairs={{8,0},{16,8},{24,16},{0,24},{9,1},{17,9},{25,17},{1,25},{10,2},{18... | collective-permute-start | bytes 786440 | tf_op jit(solution)/shard_map/ppermute | solution.py:18
  19.7 98.3 %collective-permute-start.2 = (f32[34,1,128,128]{3,2,1,0:T(8,128)S(1)}, f32[34,1,128,128]{3,2,1,0:T(8,128)S(1)}, u32[]{:S(2)}, u32[]{:S(2)}) collective-permute-start(f32[34,1,128,128]{3,2,1,0:T(8,128)S(1)} %get-tuple-element.133), channel_id=1, source_target_pairs={{0,2},{2,4},{4,6},{6,0},{1,3},{3,5},{5,7},{7,1},{8,10},{10,12},{12... | collective-permute-start | bytes 6684680 | tf_op jit(solution)/shard_map/ppermute | solution.py:16
  19.8 98.2 %collective-permute-start.3 = (f32[34,1,128,128]{3,2,1,0:T(8,128)S(1)}, f32[34,1,128,128]{3,2,1,0:T(8,128)S(1)}, u32[]{:S(2)}, u32[]{:S(2)}) collective-permute-start(f32[34,1,128,128]{3,2,1,0:T(8,128)S(1)} %get-tuple-element.134), channel_id=1, source_target_pairs={{2,0},{4,2},{6,4},{0,6},{3,1},{5,3},{7,5},{1,7},{10,8},{12,10},{14... | collective-permute-start | bytes 6684680 | tf_op jit(solution)/shard_map/ppermute | solution.py:18
  118.2 5.7 collective-permute-start.4
  119.8 5.5 collective-permute-start.5
  155.5 7.9 %collective-permute-start.6 = (f32[1,4,128,128]{3,2,1,0:T(8,128)S(1)}, f32[1,4,128,128]{3,2,1,0:T(8,128)S(1)}, u32[]{:S(2)}, u32[]{:S(2)}) collective-permute-start(f32[1,4,128,128]{3,2,1,0:T(8,128)S(1)} %get-tuple-element.139), channel_id=1, source_target_pairs={{0,8},{8,16},{16,24},{24,0},{1,9},{9,17},{17,25},{25,1},{2,10},{10... | collective-permute-start | bytes 786440 | tf_op jit(solution)/shard_map/ppermute | solution.py:16
  155.6 7.9 %collective-permute-start.7 = (f32[1,4,128,128]{3,2,1,0:T(8,128)S(1)}, f32[1,4,128,128]{3,2,1,0:T(8,128)S(1)}, u32[]{:S(2)}, u32[]{:S(2)}) collective-permute-start(f32[1,4,128,128]{3,2,1,0:T(8,128)S(1)} %get-tuple-element.140), channel_id=1, source_target_pairs={{8,0},{16,8},{24,16},{0,24},{9,1},{17,9},{25,17},{1,25},{10,2},{18... | collective-permute-start | bytes 786440 | tf_op jit(solution)/shard_map/ppermute | solution.py:18
  163.7 51.3 %collective-permute-start.8 = (f32[34,1,128,128]{3,2,1,0:T(8,128)S(1)}, f32[34,1,128,128]{3,2,1,0:T(8,128)S(1)}, u32[]{:S(2)}, u32[]{:S(2)}) collective-permute-start(f32[34,1,128,128]{3,2,1,0:T(8,128)S(1)} %get-tuple-element.131), channel_id=1, source_target_pairs={{0,2},{2,4},{4,6},{6,0},{1,3},{3,5},{5,7},{7,1},{8,10},{10,12},{12... | collective-permute-start | bytes 6684680 | tf_op jit(solution)/shard_map/ppermute | solution.py:16
  166.2 97.3 %collective-permute-start.9 = (f32[34,1,128,128]{3,2,1,0:T(8,128)S(1)}, f32[34,1,128,128]{3,2,1,0:T(8,128)S(1)}, u32[]{:S(2)}, u32[]{:S(2)}) collective-permute-start(f32[34,1,128,128]{3,2,1,0:T(8,128)S(1)} %get-tuple-element.132), channel_id=1, source_target_pairs={{2,0},{4,2},{6,4},{0,6},{3,1},{5,3},{7,5},{1,7},{10,8},{12,10},{14... | collective-permute-start | bytes 6684680 | tf_op jit(solution)/shard_map/ppermute | solution.py:18
  263.7 6.0 collective-permute-start.10
  303.8 7.5 collective-permute-start.12
  304.1 7.2 collective-permute-start.13
  311.8 51.7 %collective-permute-start.14 = (f32[34,1,128,128]{3,2,1,0:T(8,128)S(1)}, f32[34,1,128,128]{3,2,1,0:T(8,128)S(1)}, u32[]{:S(2)}, u32[]{:S(2)}) collective-permute-start(f32[34,1,128,128]{3,2,1,0:T(8,128)S(1)} %get-tuple-element.129), channel_id=1, source_target_pairs={{0,2},{2,4},{4,6},{6,0},{1,3},{3,5},{5,7},{7,1},{8,10},{10,12},{12... | collective-permute-start | bytes 6684680 | tf_op jit(solution)/shard_map/ppermute | solution.py:16
  314.6 97.3 %collective-permute-start.15 = (f32[34,1,128,128]{3,2,1,0:T(8,128)S(1)}, f32[34,1,128,128]{3,2,1,0:T(8,128)S(1)}, u32[]{:S(2)}, u32[]{:S(2)}) collective-permute-start(f32[34,1,128,128]{3,2,1,0:T(8,128)S(1)} %get-tuple-element.130), channel_id=1, source_target_pairs={{2,0},{4,2},{6,4},{0,6},{3,1},{5,3},{7,5},{1,7},{10,8},{12,10},{14... | collective-permute-start | bytes 6684680 | tf_op jit(solution)/shard_map/ppermute | solution.py:18
  413.3 6.3 collective-permute-start.16
  415.0 6.2 collective-permute-start.17
  445.7 7.6 collective-permute-start.18
  445.8 7.5 collective-permute-start.19
  456.1 99.1 %collective-permute-start.20 = (f32[34,1,128,128]{3,2,1,0:T(8,128)S(1)}, f32[34,1,128,128]{3,2,1,0:T(8,128)S(1)}, u32[]{:S(2)}, u32[]{:S(2)}) collective-permute-start(f32[34,1,128,128]{3,2,1,0:T(8,128)S(1)} %get-tuple-element.127), channel_id=1, source_target_pairs={{0,2},{2,4},{4,6},{6,0},{1,3},{3,5},{5,7},{7,1},{8,10},{10,12},{12... | collective-permute-start | bytes 6684680 | tf_op jit(solution)/shard_map/ppermute | solution.py:16
  457.6 97.6 %collective-permute-start.21 = (f32[34,1,128,128]{3,2,1,0:T(8,128)S(1)}, f32[34,1,128,128]{3,2,1,0:T(8,128)S(1)}, u32[]{:S(2)}, u32[]{:S(2)}) collective-permute-start(f32[34,1,128,128]{3,2,1,0:T(8,128)S(1)} %get-tuple-element.128), channel_id=1, source_target_pairs={{2,0},{4,2},{6,4},{0,6},{3,1},{5,3},{7,5},{1,7},{10,8},{12,10},{14... | collective-permute-start | bytes 6684680 | tf_op jit(solution)/shard_map/ppermute | solution.py:18
  557.9 6.3 collective-permute-start.22
  559.3 6.6 collective-permute-start.23
  (11 other events, 447.8 us)
Sparse Core Ops, SparseCore 0:
  600.9 145.6 all-gather.2
where the time goes:
time: 774 us; the launch traced here: 769 us
  waiting for transfers between devices  577 us (75%)
  other arithmetic  137 us (18%)
  starting transfers between devices  25.4 us (3%)
  local copies, waits for them, and re-layouts  14.8 us (2%)
  between operations  14.3 us (2%)
    ppermute x12, waiting for transfers between devices, with_halo(): lax.ppermute(tail, axis, [(i, (i + 1) % count) for i in range(count)])  329 us
    all_gather x1, waiting for transfers between devices, carried_in(): pieces = lax.all_gather(value, axis)  146 us
    add x4, other arithmetic, march_step(): return middle + 0.1 * spread + 0.2 * middle * (1.0 - middle * crowding)  109 us
    ppermute x12, waiting for transfers between devices, with_halo(): lax.ppermute(head, axis, [((i + 1) % count, i) for i in range(count)])  102 us
  transfers between devices with their start and end apart: 25, of which 19 were waited for; matrix products, arithmetic and copies ran while one was open for 1% of the time, Pallas kernels for 0%

commit v1 on v0

v1 whole, which is shorter than its diff:
```python
import functools

import jax
import jax.numpy as jnp
from jax import lax
from jax.experimental import pallas as pl
from jax.experimental.pallas import tpu as pltpu
from jax.sharding import PartitionSpec as P

STEPS = 4
CHUNKS = 16
MESH = pl.DeviceIdType.MESH
LO, HI = 0, 1


def kernel(
    sizes, density, crowding, running, density_end,
    field, crowd, lon, lev,
    load_sem, crowd_sem, store_sem,
    lon_send, lon_recv, lev_send, lev_recv, lat_send, lat_recv, credit,
):
    n_lat, n_lon, n_lev = sizes
    J, I, K, L = density.shape
    rows = max(1, J // CHUNKS)
    chunks = J // rows
    names = {"lat": n_lat, "lon": n_lon, "lev": n_lev}
    me = {name: lax.axis_index(name) for name in names}
    near = {
        name: (
            {name: lax.rem(me[name] + n - 1, n)},
            {name: lax.rem(me[name] + 1, n)},
        )
        for name, n in names.items()
    }

    def load(c):
        own = pl.ds(c * rows, rows)
        return pltpu.make_async_copy(density.at[own], field.at[0, pl.ds(1 + c * rows, rows)], load_sem.at[c])

    def load_crowd(c):
        own = pl.ds(c * rows, rows)
        return pltpu.make_async_copy(crowding.at[own], crowd.at[own], crowd_sem.at[c])

    def store(slot, c, target, which):
        return pltpu.make_async_copy(
            field.at[slot, pl.ds(1 + c * rows, rows)], target.at[pl.ds(c * rows, rows)], store_sem.at[which, c]
        )

    def lon_copy(slot, side, c):
        plane = 0 if side == LO else I - 1
        return pltpu.make_async_remote_copy(
            src_ref=field.at[slot, pl.ds(1 + c * rows, rows), plane],
            dst_ref=lon.at[1 - side, pl.ds(c * rows, rows)],
            send_sem=lon_send.at[side, c],
            recv_sem=lon_recv.at[1 - side, c],
            device_id=near["lon"][side],
            device_id_type=MESH,
        )

    def lev_copy(slot, side, c):
        first = 0 if side == LO else K - 8
        return pltpu.make_async_remote_copy(
            src_ref=field.at[slot, pl.ds(1 + c * rows, rows), :, pl.ds(first, 8)],
            dst_ref=lev.at[slot, 1 - side, pl.ds(c * rows, rows)],
            send_sem=lev_send.at[side, c],
            recv_sem=lev_recv.at[slot, 1 - side, c],
            device_id=near["lev"][side],
            device_id_type=MESH,
        )

    def lat_copy(slot, side):
        return pltpu.make_async_remote_copy(
            src_ref=field.at[slot, 1 if side == LO else J],
            dst_ref=field.at[slot, J + 1 if side == LO else 0],
            send_sem=lat_send.at[side],
            recv_sem=lat_recv.at[slot, 1 - side],
            device_id=near["lat"][side],
            device_id_type=MESH,
        )

    def at_edges(c, act):
        @pl.when(c == 0)
        def _():
            act(LO)

        @pl.when(c == chunks - 1)
        def _():
            act(HI)

    def start_sends(slot, c):
        for side in (LO, HI):
            lon_copy(slot, side, c).start()
            lev_copy(slot, side, c).start()
        at_edges(c, lambda side: lat_copy(slot, side).start())

    def end_sends(slot, c):
        for side in (LO, HI):
            lon_copy(slot, side, c).wait_send()
            lev_copy(slot, side, c).wait_send()
        at_edges(c, lambda side: lat_copy(slot, side).wait_send())

    def end_receives(slot, c):
        for side in (LO, HI):
            lon_copy(slot, side, c).wait_recv()
            lev_copy(slot, side, c).wait_recv()
        at_edges(c, lambda side: lat_copy(slot, 1 - side).wait_recv())

    def give_credit(side, c):
        pl.semaphore_signal(
            credit.at[1 - side, c], inc=1, device_id=near["lon"][side], device_id_type=MESH
        )

    def loop(count, act):
        def lap(c, carry):
            act(c)
            return carry

        lax.fori_loop(0, count, lap, 0)

    def begin(c):
        load(c).start()

    def begin_crowd(c):
        load_crowd(c).start()

    loop(chunks, begin)
    loop(chunks, begin_crowd)

    barrier = pltpu.get_barrier_semaphore()
    for name in names:
        for side in (LO, HI):
            pl.semaphore_signal(barrier, inc=1, device_id=near[name][side], device_id_type=MESH)
    pl.semaphore_wait(barrier, 2 * len(names))

    def first(c):
        load(c).wait()
        start_sends(0, c)

    loop(chunks, first)

    at_k = lax.broadcasted_iota(jnp.int32, (K, L), 0)

    def advance(slot, j):
        for i in range(I):
            middle = field[slot, j + 1, i]
            below = lon[LO, j] if i == 0 else field[slot, j + 1, i - 1]
            above = lon[HI, j] if i == I - 1 else field[slot, j + 1, i + 1]
            before = jnp.where(at_k == 0, lev[slot, LO, j, i, 7:8], pltpu.roll(middle, 1, 0))
            after = jnp.where(at_k == K - 1, lev[slot, HI, j, i, 0:1], pltpu.roll(middle, K - 1, 0))
            around = (field[slot, j, i] + field[slot, j + 2, i]) + (below + above) + (before + after)
            field[1 - slot, j + 1, i] = middle * (0.6 - 0.2 * (middle * crowd[j, i])) + 0.1 * around

    for step in range(STEPS):
        slot = step % 2
        last = step == STEPS - 1

        def march(c):
            if step == 0:
                load_crowd(c).wait()
            end_receives(slot, c)
            loop(rows, lambda r: advance(slot, c * rows + r))
            give_credit(LO, c)
            if not last:
                give_credit(HI, c)
            end_sends(slot, c)
            if last:
                store(1 - slot, c, density_end, 0).start()
            else:
                pl.semaphore_wait(credit.at[LO, c], 1)
                pl.semaphore_wait(credit.at[HI, c], 1)
                start_sends(1 - slot, c)

        loop(chunks, march)

    done, spare = STEPS % 2, 1 - STEPS % 2
    share = 1.0 / (I * n_lon)

    def total(j):
        so_far = jnp.where(me["lon"] > 0, lon[LO, j], 0.0)
        for i in range(I):
            so_far = so_far + field[done, j + 1, i] * share
            field[spare, j + 1, i] = so_far

    def add_up(c):
        @pl.when(me["lon"] > 0)
        def _():
            lon_copy(spare, HI, c).wait_recv()

        loop(rows, lambda r: total(c * rows + r))
        pl.semaphore_wait(credit.at[HI, c], 1)

        @pl.when(me["lon"] < n_lon - 1)
        def _():
            lon_copy(spare, HI, c).start()

        store(spare, c, running, 1).start()

    loop(chunks, add_up)

    def finish(c):
        @pl.when(me["lon"] < n_lon - 1)
        def _():
            lon_copy(spare, HI, c).wait_send()

        store(done, c, density_end, 0).wait()
        store(spare, c, running, 1).wait()

    loop(chunks, finish)


def body(sizes, density, crowding):
    J, I, K, L = density.shape
    chunks = J // max(1, J // CHUNKS)
    shape = jax.ShapeDtypeStruct(density.shape, jnp.float32)
    dma = pltpu.SemaphoreType.DMA
    return pl.pallas_call(
        functools.partial(kernel, sizes),
        out_shape=(shape, shape),
        in_specs=[pl.BlockSpec(memory_space=pl.ANY)] * 2,
        out_specs=(pl.BlockSpec(memory_space=pl.ANY),) * 2,
        scratch_shapes=[
            pltpu.VMEM((2, J + 2, I, K, L), jnp.float32),
            pltpu.VMEM((J, I, K, L), jnp.float32),
            pltpu.VMEM((2, J, K, L), jnp.float32),
            pltpu.VMEM((2, 2, J, I, 8, L), jnp.float32),
            dma((chunks,)),
            dma((chunks,)),
            dma((2, chunks)),
            dma((2, chunks)),
            dma((2, chunks)),
            dma((2, chunks)),
            dma((2, 2, chunks)),
            dma((2,)),
            dma((2, 2)),
            pltpu.SemaphoreType.REGULAR((2, chunks)),
        ],
        compiler_params=pltpu.CompilerParams(
            collective_id=0, has_side_effects=True, vmem_limit_bytes=67043328
        ),
    )(density, crowding)


def solution(mesh):
    sizes = tuple(mesh.shape[name] for name in ("lat", "lon", "lev"))
    return jax.shard_map(
        functools.partial(body, sizes),
        mesh=mesh,
        in_specs=(P("lat", "lon", "lev", None), P("lat", "lon", "lev", None)),
        out_specs=(P("lat", "lon", "lev", None), P("lat", "lon", "lev", None)),
        check_vma=False,
    )
```

time: 774 us -> 439 us (0.57)
  waiting for transfers between devices: 577 us -> 0 us
  Pallas kernels: 0 us -> 427 us
  other arithmetic: 137 us -> 0 us
  starting transfers between devices: 25.4 us -> 0 us
  between operations: 14.3 us -> 0.65 us
    ppermute x24 -> x0, waiting for transfers between devices: 431 us -> none  [the longest x12 329 us: with_halo(): lax.ppermute(tail, axis, [(i, (i + 1) % count) for i in range(count)])]
    pallas_call x0 -> x1, Pallas kernels: none -> 427 us  [body(): pl.pallas_call(functools.partial(kernel, sizes), out_shape=(shape, shape)...]
    all_gather x1 -> x0, waiting for transfers between devices: 146 us -> none  [carried_in(): pieces = lax.all_gather(value, axis)]
    add x4 -> x0, other arithmetic: 109 us -> none  [march_step(): return middle + 0.1 * spread + 0.2 * middle * (1.0 - middle * crowding)]
    ppermute x24 -> x0, starting transfers between devices: 25.3 us -> none  [the longest x12 13.6 us: with_halo(): lax.ppermute(tail, axis, [(i, (i + 1) % count) for i in range(count)])]
    div x1 -> x0, other arithmetic: 8.71 us -> none  [body(): running_total = (here + below) / (density.shape[1] * lax.axis_size('lon'))]
    another operation x1 -> x0, other arithmetic: 8.36 us -> none  [body(): here = jnp.cumsum(density, axis=1)]
  transfers between devices with their start and end apart: 25 -> 0, of which waited for: 19 -> 0; matrix products, arithmetic and copies ran while one was open for 1% -> 0% of each run, Pallas kernels for 0% -> 0%
where the time goes in v1:
time: 439 us
  Pallas kernels  427 us (97%)
  local copies, waits for them, and re-layouts  11.4 us (3%)
    pallas_call x1, Pallas kernels, body(): pl.pallas_call(functools.partial(kernel, sizes), out_shape=(shape, shape)...  427 us
    unnamed x4, local copies, waits for them, and re-layouts  11.4 us

profile of v1, /device:TPU:24, one launch (start us, length us, event | category | flops | bytes accessed | tf_op | source)
XLA Modules:
  0.0 438.7 jit_solution(3941556437158359668)
XLA Ops:
  0.6 426.6 %shard_map.41 = (f32[32,4,128,128]{3,2,1,0:T(8,128)}, f32[32,4,128,128]{3,2,1,0:T(8,128)}) custom-call(f32[32,4,128,128]{3,2,1,0:T(8,128)} %density.1, f32[32,4,128,128]{3,2,1,0:T(8,128)} %crowding.1), custom_call_target="tpu_custom_call" | custom-call | tf_op jit(solution)/shard_map/pallas_call | solution.py:216
  427.2 0.0 copy-start
  427.2 8.0 %copy.6 = f32[32,4,128,128]{3,2,1,0:T(8,128)} copy(f32[32,4,128,128]{3,2,1,0:T(8,128)} %get-tuple-element.4) | data formatting | bytes 16777216
  435.3 0.0 copy-done
  435.3 3.4 copy.7
Async XLA Ops:
  427.2 8.1 %copy-start = (f32[32,4,128,128]{3,2,1,0:T(8,128)S(1)}, f32[32,4,128,128]{3,2,1,0:T(8,128)}, u32[]{:S(2)}) copy-start(f32[32,4,128,128]{3,2,1,0:T(8,128)} %get-tuple-element.5) | copy-start | bytes 25165828

commit v2 on v1

--- a/solution.py
+++ b/solution.py
@@ -8,7 +8,8 @@
 from jax.sharding import PartitionSpec as P
 
 STEPS = 4
-CHUNKS = 16
+CHUNKS = 32
+LAG = 2
 MESH = pl.DeviceIdType.MESH
 LO, HI = 0, 1
 
@@ -123,13 +124,11 @@
     def begin_crowd(c):
         load_crowd(c).start()
 
-    loop(chunks, begin)
-    loop(chunks, begin_crowd)
-
     barrier = pltpu.get_barrier_semaphore()
     for name in names:
         for side in (LO, HI):
             pl.semaphore_signal(barrier, inc=1, device_id=near[name][side], device_id_type=MESH)
+    loop(chunks, begin)
     pl.semaphore_wait(barrier, 2 * len(names))
 
     def first(c):
@@ -137,6 +136,7 @@
         start_sends(0, c)
 
     loop(chunks, first)
+    loop(chunks, begin_crowd)
 
     at_k = lax.broadcasted_iota(jnp.int32, (K, L), 0)
 
@@ -149,6 +149,30 @@
             after = jnp.where(at_k == K - 1, lev[slot, HI, j, i, 0:1], pltpu.roll(middle, K - 1, 0))
             around = (field[slot, j, i] + field[slot, j + 2, i]) + (below + above) + (before + after)
             field[1 - slot, j + 1, i] = middle * (0.6 - 0.2 * (middle * crowd[j, i])) + 0.1 * around
+
+    done, spare = STEPS % 2, 1 - STEPS % 2
+    lag = min(LAG, chunks)
+    share = 1.0 / (I * n_lon)
+
+    def total(j):
+        so_far = jnp.where(me["lon"] > 0, lon[LO, j], 0.0)
+        for i in range(I):
+            so_far = so_far + field[done, j + 1, i] * share
+            field[spare, j + 1, i] = so_far
+
+    def add_up(c):
+        @pl.when(me["lon"] > 0)
+        def _():
+            lon_copy(spare, HI, c).wait_recv()
+
+        loop(rows, lambda r: total(c * rows + r))
+        pl.semaphore_wait(credit.at[HI, c], 1)
+
+        @pl.when(me["lon"] < n_lon - 1)
+        def _():
+            lon_copy(spare, HI, c).start()
+
+        store(spare, c, running, 1).start()
 
     for step in range(STEPS):
         slot = step % 2
@@ -165,6 +189,10 @@
             end_sends(slot, c)
             if last:
                 store(1 - slot, c, density_end, 0).start()
+
+                @pl.when(c >= lag)
+                def _():
+                    add_up(c - lag)
             else:
                 pl.semaphore_wait(credit.at[LO, c], 1)
                 pl.semaphore_wait(credit.at[HI, c], 1)
@@ -172,30 +200,7 @@
 
         loop(chunks, march)
 
-    done, spare = STEPS % 2, 1 - STEPS % 2
-    share = 1.0 / (I * n_lon)
-
-    def total(j):
-        so_far = jnp.where(me["lon"] > 0, lon[LO, j], 0.0)
-        for i in range(I):
-            so_far = so_far + field[done, j + 1, i] * share
-            field[spare, j + 1, i] = so_far
-
-    def add_up(c):
-        @pl.when(me["lon"] > 0)
-        def _():
-            lon_copy(spare, HI, c).wait_recv()
-
-        loop(rows, lambda r: total(c * rows + r))
-        pl.semaphore_wait(credit.at[HI, c], 1)
-
-        @pl.when(me["lon"] < n_lon - 1)
-        def _():
-            lon_copy(spare, HI, c).start()
-
-        store(spare, c, running, 1).start()
-
-    loop(chunks, add_up)
+    loop(lag, lambda c: add_up(chunks - lag + c))
 
     def finish(c):
         @pl.when(me["lon"] < n_lon - 1)

time: 439 us -> 440 us (level)
  no operation moved by 1% of the time
where the time goes in v2:
time: 440 us
  Pallas kernels  428 us (97%)
  local copies, waits for them, and re-layouts  11.4 us (3%)
    pallas_call x1, Pallas kernels, body(): pl.pallas_call(functools.partial(kernel, sizes), out_shape=(shape, shape)...  428 us
    unnamed x4, local copies, waits for them, and re-layouts  11.4 us

profile of v2, /device:TPU:24, one launch (start us, length us, event | category | flops | bytes accessed | tf_op | source)
XLA Modules:
  0.0 440.0 jit_solution(2131285805886139766)
XLA Ops:
  0.6 428.0 %shard_map.41 = (f32[32,4,128,128]{3,2,1,0:T(8,128)}, f32[32,4,128,128]{3,2,1,0:T(8,128)}) custom-call(f32[32,4,128,128]{3,2,1,0:T(8,128)} %density.1, f32[32,4,128,128]{3,2,1,0:T(8,128)} %crowding.1), custom_call_target="tpu_custom_call" | custom-call | tf_op jit(solution)/shard_map/pallas_call | solution.py:221
  428.6 0.0 copy-start
  428.6 8.0 %copy.6 = f32[32,4,128,128]{3,2,1,0:T(8,128)} copy(f32[32,4,128,128]{3,2,1,0:T(8,128)} %get-tuple-element.4) | data formatting | bytes 16777216
  436.6 0.0 copy-done
  436.7 3.4 copy.7
Async XLA Ops:
  428.6 8.1 %copy-start = (f32[32,4,128,128]{3,2,1,0:T(8,128)S(1)}, f32[32,4,128,128]{3,2,1,0:T(8,128)}, u32[]{:S(2)}) copy-start(f32[32,4,128,128]{3,2,1,0:T(8,128)} %get-tuple-element.5) | copy-start | bytes 25165828

commit v3 on v2

--- a/solution.py
+++ b/solution.py
@@ -8,8 +8,7 @@
 from jax.sharding import PartitionSpec as P
 
 STEPS = 4
-CHUNKS = 32
-LAG = 2
+CHUNKS = 16
 MESH = pl.DeviceIdType.MESH
 LO, HI = 0, 1
 
@@ -17,7 +16,7 @@
 def kernel(
     sizes, density, crowding, running, density_end,
     field, crowd, lon, lev,
-    load_sem, crowd_sem, store_sem,
+    load_sem, crowd_sem,
     lon_send, lon_recv, lev_send, lev_recv, lat_send, lat_recv, credit,
 ):
     n_lat, n_lon, n_lev = sizes
@@ -42,11 +41,6 @@
         own = pl.ds(c * rows, rows)
         return pltpu.make_async_copy(crowding.at[own], crowd.at[own], crowd_sem.at[c])
 
-    def store(slot, c, target, which):
-        return pltpu.make_async_copy(
-            field.at[slot, pl.ds(1 + c * rows, rows)], target.at[pl.ds(c * rows, rows)], store_sem.at[which, c]
-        )
-
     def lon_copy(slot, side, c):
         plane = 0 if side == LO else I - 1
         return pltpu.make_async_remote_copy(
@@ -58,6 +52,17 @@
             device_id_type=MESH,
         )
 
+    def total_copy(c):
+        own = pl.ds(c * rows, rows)
+        return pltpu.make_async_remote_copy(
+            src_ref=running.at[own, I - 1],
+            dst_ref=lon.at[LO, own],
+            send_sem=lon_send.at[HI, c],
+            recv_sem=lon_recv.at[LO, c],
+            device_id=near["lon"][HI],
+            device_id_type=MESH,
+        )
+
     def lev_copy(slot, side, c):
         first = 0 if side == LO else K - 8
         return pltpu.make_async_remote_copy(
@@ -140,7 +145,7 @@
 
     at_k = lax.broadcasted_iota(jnp.int32, (K, L), 0)
 
-    def advance(slot, j):
+    def advance(slot, j, put):
         for i in range(I):
             middle = field[slot, j + 1, i]
             below = lon[LO, j] if i == 0 else field[slot, j + 1, i - 1]
@@ -148,67 +153,60 @@
             before = jnp.where(at_k == 0, lev[slot, LO, j, i, 7:8], pltpu.roll(middle, 1, 0))
             after = jnp.where(at_k == K - 1, lev[slot, HI, j, i, 0:1], pltpu.roll(middle, K - 1, 0))
             around = (field[slot, j, i] + field[slot, j + 2, i]) + (below + above) + (before + after)
-            field[1 - slot, j + 1, i] = middle * (0.6 - 0.2 * (middle * crowd[j, i])) + 0.1 * around
-
-    done, spare = STEPS % 2, 1 - STEPS % 2
-    lag = min(LAG, chunks)
+            put(j, i, middle * (0.6 - 0.2 * (middle * crowd[j, i])) + 0.1 * around)
+
     share = 1.0 / (I * n_lon)
 
     def total(j):
         so_far = jnp.where(me["lon"] > 0, lon[LO, j], 0.0)
         for i in range(I):
-            so_far = so_far + field[done, j + 1, i] * share
-            field[spare, j + 1, i] = so_far
+            so_far = so_far + density_end[j, i] * share
+            running[j, i] = so_far
 
     def add_up(c):
         @pl.when(me["lon"] > 0)
         def _():
-            lon_copy(spare, HI, c).wait_recv()
+            total_copy(c).wait_recv()
 
         loop(rows, lambda r: total(c * rows + r))
         pl.semaphore_wait(credit.at[HI, c], 1)
 
         @pl.when(me["lon"] < n_lon - 1)
         def _():
-            lon_copy(spare, HI, c).start()
-
-        store(spare, c, running, 1).start()
+            total_copy(c).start()
 
     for step in range(STEPS):
         slot = step % 2
         last = step == STEPS - 1
+
+        def put(j, i, value):
+            if last:
+                density_end[j, i] = value
+            else:
+                field[1 - slot, j + 1, i] = value
 
         def march(c):
             if step == 0:
                 load_crowd(c).wait()
             end_receives(slot, c)
-            loop(rows, lambda r: advance(slot, c * rows + r))
+            loop(rows, lambda r: advance(slot, c * rows + r, put))
             give_credit(LO, c)
             if not last:
                 give_credit(HI, c)
             end_sends(slot, c)
-            if last:
-                store(1 - slot, c, density_end, 0).start()
-
-                @pl.when(c >= lag)
-                def _():
-                    add_up(c - lag)
-            else:
+            if not last:
                 pl.semaphore_wait(credit.at[LO, c], 1)
                 pl.semaphore_wait(credit.at[HI, c], 1)
                 start_sends(1 - slot, c)
 
         loop(chunks, march)
 
-    loop(lag, lambda c: add_up(chunks - lag + c))
+    loop(chunks, add_up)
 
     def finish(c):
         @pl.when(me["lon"] < n_lon - 1)
         def _():
-            lon_copy(spare, HI, c).wait_send()
-
-        store(done, c, density_end, 0).wait()
-        store(spare, c, running, 1).wait()
+            total_copy(c).wait_send()
 
     loop(chunks, finish)
 
@@ -216,13 +214,13 @@
 def body(sizes, density, crowding):
     J, I, K, L = density.shape
     chunks = J // max(1, J // CHUNKS)
-    shape = jax.ShapeDtypeStruct(density.shape, jnp.float32)
+    shape = pltpu.VMEM(density.shape, jnp.float32)
     dma = pltpu.SemaphoreType.DMA
     return pl.pallas_call(
         functools.partial(kernel, sizes),
         out_shape=(shape, shape),
         in_specs=[pl.BlockSpec(memory_space=pl.ANY)] * 2,
-        out_specs=(pl.BlockSpec(memory_space=pl.ANY),) * 2,
+        out_specs=(pl.BlockSpec(memory_space=pltpu.VMEM),) * 2,
         scratch_shapes=[
             pltpu.VMEM((2, J + 2, I, K, L), jnp.float32),
             pltpu.VMEM((J, I, K, L), jnp.float32),
@@ -233,14 +231,13 @@
             dma((2, chunks)),
             dma((2, chunks)),
             dma((2, chunks)),
-            dma((2, chunks)),
             dma((2, 2, chunks)),
             dma((2,)),
             dma((2, 2)),
             pltpu.SemaphoreType.REGULAR((2, chunks)),
         ],
         compiler_params=pltpu.CompilerParams(
-            collective_id=0, has_side_effects=True, vmem_limit_bytes=67043328
+            collective_id=0, has_side_effects=True, vmem_limit_bytes=40 * 2**20
         ),
     )(density, crowding)
 

time: 440 us -> 433 us (0.984)
  local copies, waits for them, and re-layouts: 11.4 us -> 6.8 us
    unnamed x4 -> x2, local copies, waits for them, and re-layouts: 11.4 us -> 6.8 us
where the time goes in v3:
time: 433 us
  Pallas kernels  425 us (98%)
  local copies, waits for them, and re-layouts  6.8 us (2%)
    pallas_call x1, Pallas kernels, body(): pl.pallas_call(functools.partial(kernel, sizes), out_shape=(shape, shape)...  425 us

profile of v3, /device:TPU:24, one launch (start us, length us, event | category | flops | bytes accessed | tf_op | source)
XLA Modules:
  0.0 432.8 jit_solution(5284405992971748774)
XLA Ops:
  0.6 425.4 %shard_map.41 = (f32[32,4,128,128]{3,2,1,0:T(8,128)S(1)}, f32[32,4,128,128]{3,2,1,0:T(8,128)S(1)}) custom-call(f32[32,4,128,128]{3,2,1,0:T(8,128)} %density.1, f32[32,4,128,128]{3,2,1,0:T(8,128)} %crowding.1), custom_call_target="tpu_custom_call" | custom-call | tf_op jit(solution)/shard_map/pallas_call | solution.py:219
  426.0 3.4 copy.6
  429.4 3.4 copy.7
